TPU v7x, 256 devices: a whole 4x4x8 slice. The times are simulated.
256 devices in a mesh: section: 8 (over z), ctx: 32 (over x, y, core).
Axes of the slice: x: 4, y: 4, z: 8, core: 2. Of those that a mesh axis runs over, the one named last changes fastest.
Arguments:
- queries: bfloat16 [8, 8192, 3072], P('section', 'ctx'), may hold values from -160 to 160
- keys: bfloat16 [8, 8192, 512], P('section', 'ctx'), may hold values from -48 to 48
- values: bfloat16 [8, 8192, 512], P('section', 'ctx'), may hold values from -15 to 15
- cotangent: bfloat16 [8, 8192, 3072], P('section', 'ctx'), may hold values from -6 to 6
- router_logits: bfloat16 [8, 8192], P('section', 'ctx'), may hold values from -8 to 8
- positions: int32 [8, 8192], P('section', 'ctx'), may hold values from -1 to 32767, as said below
- counts: int32 [8, 32], P('section', 'ctx'), may hold values from 0 to 2, as said below
Outputs:
- handed: bfloat16 [8, 8192, 3072], P('section', 'ctx')
- value_grad: bfloat16 [8, 8192, 512], P('section', 'ctx')
- gate_grad: bfloat16 [8, 8192], P('section', 'ctx')
Inputs may be any that keep to these rules, and one draw needn't show every extreme that they name: For every micro-batch and every shard c, the counts of shards 0 to c sum to c + 1 or c + 2; shard 0 holds 2 blocks; all counts of a micro-batch sum to 32. In shard c's slots, the first counts * 128 hold distinct positions in increasing order, all within c * 1024 to (c + 1) * 1024 - 1; the other slots hold -1.
All inputs are finite; a program needn't handle non-finite values.
Results may differ from a plain program's by a relative error of at most 0.0066.
Values may be sent and summed in bfloat16 or wider, within the bound.
A program may use at most 128 MiB of HBM per device.

v0:
```python
import math
import jax
import jax.numpy as jnp
from jax import lax
from jax.sharding import PartitionSpec as P

QUERY_HEADS = 24
KEY_VALUE_HEADS = 4
HEAD_SIZE = 128
BLOCK_ROWS = 128
MAXB = 2
score_masked_out = -1e30


def copy_for_each(x, axis):
    copies = jnp.broadcast_to(x, (lax.axis_size(axis), *x.shape))
    return lax.all_to_all(copies, axis, split_axis=0, concat_axis=0, tiled=True)


def folded_in_pairs(pieces, combine):
    while len(jax.tree.leaves(pieces)[0]) > 1:
        pieces = jax.vmap(combine)(*(pieces[side::2] for side in (0, 1)))
    return pieces[0]


def carried_in(x, axis, combine, identity):
    devices, mine = (lax.axis_size(axis), lax.axis_index(axis))
    passed = jnp.arange(devices) < mine

    def kept(part, zero, own):
        part = jnp.where(
            passed.reshape(-1, *(1 for _ in own.shape)), part, jnp.asarray(zero, own.dtype)
        )
        return part

    pieces = copy_for_each(x, axis)
    return folded_in_pairs(kept(pieces, identity, x), combine)


def passed_along(block, axis, distance):
    devices = range(lax.axis_size(axis))
    route = [(i - distance, i) for i in devices if i - distance in devices]
    return lax.ppermute(block, axis, route)


def sent_together(arrays, axis, dim, along):
    widths = [a.shape[along] for a in arrays]
    both = jnp.concatenate(arrays, axis=along)
    out = lax.all_gather(both, axis, axis=dim, tiled=True)
    return tuple(jnp.split(out, [sum(widths[:k]) for k in range(1, len(widths))], axis=along))


def for_sending(x):

    def short(part):
        return part.astype(jnp.bfloat16) if part.dtype == jnp.float32 else part

    return jax.tree.map(short, x)


def in_blocks(x, dim, devices):
    before, after = (x.shape[:dim], x.shape[dim + 1 :])
    return jnp.moveaxis(x.reshape(*before, devices, -1, *after), dim, 0)


def sent_and_summed(x, axis, dim):
    devices = lax.axis_size(axis)
    tiles = lax.all_to_all(in_blocks(x, dim, devices), axis, 0, 0, tiled=True)
    return jnp.sum(tiles.astype(jnp.float32), axis=0)


def from_behind(x, axis, by):
    devices = lax.axis_size(axis)
    return lax.ppermute(x, axis, [(i, (i + by) % devices) for i in range(devices)])


def add_ints(earlier, later):
    return earlier + later


def local(queries, keys, values, cotangent, router_logits, positions, counts):
    query_group_width = QUERY_HEADS // KEY_VALUE_HEADS
    shards = lax.axis_size("ctx")
    key_width = BLOCK_ROWS * min(shards, max(1, 512 // BLOCK_ROWS))
    score_scale = 1.0 / math.sqrt(HEAD_SIZE)
    blocks_held = counts[0, 0]
    before = carried_in(blocks_held - 1, "ctx", add_ints, jnp.int32(0))
    carried = before + blocks_held - 1
    last_block = jnp.maximum(blocks_held - 1, 0)
    own_arrays = (queries[0], keys[0], values[0], cotangent[0], router_logits[0], positions[0])
    outgoing = [
        lax.dynamic_slice_in_dim(source, last_block * BLOCK_ROWS, BLOCK_ROWS, 0)
        for source in own_arrays
    ]
    incoming = passed_along(
        (outgoing[0], outgoing[1], outgoing[2], outgoing[3], outgoing[4], outgoing[5]), "ctx", 1
    )
    received_one = before == 1
    chosen = [
        jnp.where(received_one, arriving, source[:BLOCK_ROWS])
        for arriving, source in zip(incoming, own_arrays)
    ]
    query_row_block, key_row_block, value_rows, grad_rows, logit_rows, place_rows = chosen
    gate_values = jax.nn.sigmoid(logit_rows.astype(jnp.float32))
    query_head_rows = query_row_block.reshape(
        BLOCK_ROWS, KEY_VALUE_HEADS, query_group_width, HEAD_SIZE
    )
    latest_query = jnp.max(place_rows)

    def split_width():
        return key_width

    def scores_for(key_portion, place_part):
        local_row_count = key_portion.shape[0]
        scores = (
            jnp.einsum(
                "qhgd,khd->hgqk",
                query_head_rows,
                key_portion.reshape(local_row_count, KEY_VALUE_HEADS, HEAD_SIZE),
                preferred_element_type=jnp.float32,
            )
            * score_scale
        )
        allowed = place_part[None, :] <= place_rows[:, None]
        return (scores, allowed)

    def absorb_part(running, key_portion, value_portion, place_part):
        row_top, weight_sum, summed = running
        local_row_count = key_portion.shape[0]
        scores, allowed = scores_for(key_portion, place_part)
        new_top = jnp.maximum(
            row_top, jnp.max(jnp.where(allowed, scores, score_masked_out), axis=-1)
        )
        weights = jnp.where(allowed, jnp.exp(scores - new_top[..., None]), 0.0)
        factor = jnp.exp(row_top - new_top)
        weight_sum = weight_sum * factor + jnp.sum(weights, axis=-1)
        summed = summed * factor[..., None] + jnp.einsum(
            "hgqk,khd->hgqd",
            weights.astype(jnp.bfloat16),
            value_portion.reshape(local_row_count, KEY_VALUE_HEADS, HEAD_SIZE),
            preferred_element_type=jnp.float32,
        )
        return (new_top, weight_sum, summed)

    def absorb(running, key_portion, value_portion, place_part):
        return lax.cond(
            jnp.min(place_part) > latest_query,
            lambda: running,
            lambda: absorb_part(running, key_portion, value_portion, place_part),
        )

    start_state = (
        jnp.full((KEY_VALUE_HEADS, query_group_width, BLOCK_ROWS), score_masked_out, jnp.float32),
        jnp.zeros((KEY_VALUE_HEADS, query_group_width, BLOCK_ROWS), jnp.float32),
        jnp.zeros((KEY_VALUE_HEADS, query_group_width, BLOCK_ROWS, HEAD_SIZE), jnp.float32),
    )
    collected_rows = (
        *sent_together((key_row_block, value_rows), "ctx", 0, 1),
        lax.all_gather(for_sending(place_rows), "ctx", axis=0, tiled=True).astype(place_rows.dtype),
    )
    key_complete = collected_rows[0]
    local_row_count = key_complete.shape[0]
    rows_per_step = split_width()
    relay_step_count = local_row_count // rows_per_step
    stacked = (
        key_complete.reshape(relay_step_count, rows_per_step, KEY_VALUE_HEADS * HEAD_SIZE),
        collected_rows[1].reshape(relay_step_count, rows_per_step, KEY_VALUE_HEADS * HEAD_SIZE),
        collected_rows[2].reshape(relay_step_count, rows_per_step),
    )

    def visit(state_in, member):
        return (absorb(state_in, member[0], member[1], member[2]), None)

    final_state = lax.scan(visit, start_state, stacked)[0]
    row_top, weight_sum, summed = final_state
    attended = jnp.transpose(summed / weight_sum[..., None], (2, 0, 1, 3)).reshape(
        BLOCK_ROWS, QUERY_HEADS * HEAD_SIZE
    )
    log_total = row_top + jnp.log(weight_sum)
    gradient_broad = grad_rows.astype(jnp.float32)
    output_gradient = (
        (gate_values[:, None] * gradient_broad)
        .astype(jnp.bfloat16)
        .reshape(BLOCK_ROWS, KEY_VALUE_HEADS, query_group_width, HEAD_SIZE)
    )

    def value_portion(key_portion, place_part):
        local_row_count = key_portion.shape[0]
        scores, allowed = scores_for(key_portion, place_part)
        probabilities = jnp.where(allowed, jnp.exp(scores - log_total[..., None]), 0.0).astype(
            jnp.bfloat16
        )
        return jnp.einsum(
            "hgqk,qhgd->khd", probabilities, output_gradient, preferred_element_type=jnp.float32
        ).reshape(local_row_count, KEY_VALUE_HEADS * HEAD_SIZE)

    def value_block(key_portion, place_part):
        return lax.cond(
            jnp.min(place_part) > latest_query,
            lambda: jnp.zeros((key_portion.shape[0], KEY_VALUE_HEADS * HEAD_SIZE), jnp.float32),
            lambda: value_portion(key_portion, place_part),
        )

    key_portion = collected_rows[0]
    place_part = collected_rows[2]
    local_row_count = key_portion.shape[0]
    rows_per_step = split_width()
    relay_step_count = local_row_count // rows_per_step
    product_terms = lax.map(
        lambda member: value_block(member[0], member[1]),
        (
            key_portion.reshape(relay_step_count, rows_per_step, KEY_VALUE_HEADS * HEAD_SIZE),
            place_part.reshape(relay_step_count, rows_per_step),
        ),
    )
    value_sum = sent_and_summed(
        product_terms.reshape(local_row_count, KEY_VALUE_HEADS * HEAD_SIZE).astype(jnp.bfloat16),
        "ctx",
        0,
    )
    branch = (gate_values[:, None] * attended).astype(jnp.bfloat16)
    gate_term = (
        gate_values * (1.0 - gate_values) * jnp.sum(gradient_broad * attended, axis=1)
    ).astype(jnp.bfloat16)
    value_finished = value_sum.astype(jnp.bfloat16)
    returned = passed_along((branch, value_finished, gate_term), "ctx", -1)
    local_results = (branch, value_finished, gate_term)
    slot_lists = ([], [], [])
    for slot_index in range(MAXB):
        local_slot = jnp.logical_and(before == 0, slot_index == 0)
        back_slot = jnp.logical_and(carried == 1, blocks_held - 1 == slot_index)
        for member_index in range(3):
            mine = local_results[member_index]
            filled = jnp.where(
                local_slot, mine, jnp.where(back_slot, returned[member_index], jnp.zeros_like(mine))
            )
            slot_lists[member_index].append(filled)
    owner_branch = jnp.concatenate(slot_lists[0], axis=0)
    value_grad = jnp.concatenate(slot_lists[1], axis=0)
    gate_grad = jnp.concatenate(slot_lists[2], axis=0)
    handed = from_behind(owner_branch, "section", 1)
    return (handed[None], value_grad[None], gate_grad[None])


def solution(mesh):
    return jax.shard_map(
        local,
        mesh=mesh,
        in_specs=(
            P("section", "ctx", None),
            P("section", "ctx", None),
            P("section", "ctx", None),
            P("section", "ctx", None),
            P("section", "ctx"),
            P("section", "ctx"),
            P("section", "ctx"),
        ),
        out_specs=(P("section", "ctx", None), P("section", "ctx", None), P("section", "ctx")),
        check_vma=False,
    )
```

profile of v0, /device:TPU:2, one launch (start us, length us, event | category | flops | bytes accessed | tf_op | source)
XLA Modules:
  0.0 349.3 jit_solution(6655201932795278297)
XLA Ops:
  8.4 7.6 %all-to-all-start = ((s32[32,1,1]{2,1,0:T(1,128)}), s32[32,1,1]{2,1,0:T(1,128)S(1)}, u32[]{:S(2)}, u32[]{:S(2)}) async-start(s32[32,1,1]{2,1,0:T(1,128)} %broadcast_in_dim.73), calls=%async_computation | async-start | bytes 32768 | tf_op jit(solution)/shard_map/all_to_all | solution.py:17
  17.0 2.0 collective-permute-start.3
  20.0 3.4 collective-permute-start.2
  30.1 2.2 fusion.39
  33.4 1.9 collective-permute-start.4
  35.4 2.8 collective-permute-start.1
  39.4 1.9 collective-permute-start.7
  41.3 3.2 collective-permute-start
  45.3 5.1 %collective-permute-done.1 = s32[128]{0:T(128)S(1)} collective-permute-done((s32[128]{0:T(128)S(1)}, s32[128]{0:T(128)S(1)}, u32[]{:S(2)}, u32[]{:S(2)}) %collective-permute-start.1) | collective-permute-done | bytes 544 | tf_op jit(solution)/shard_map/ppermute | solution.py:43
  51.0 21.7 %all-gather = s32[32,1,128]{2,1,0:T(1,128)S(1)} all-gather(s32[1,1,128]{2,1,0:T(1,128)S(1)} %bitcast.117), channel_id=1, replica_groups=mesh['section'=8,'ctx'=32] {'ctx'}, dimensions={0}, use_global_device_ids=true | all-gather | bytes 16896 | tf_op jit(solution)/shard_map/all_gather | solution.py:159
  73.9 1.2 bitcast_select_fusion.2
  75.5 19.5 %all-gather.3.cloned.1.call-done = bf16[4096,1024]{1,0:T(8,128)(2,1)} async-done(((bf16[128,1024]{1,0:T(8,128)(2,1)}), bf16[4096,1024]{1,0:T(8,128)(2,1)}) %all-gather.3.cloned.1.call-update) | async-done | bytes 8388624 | tf_op jit(solution)/shard_map/all_gather | solution.py:49
  95.0 5.8 %fusion.38 = (bf16[4096,512]{1,0:T(8,128)(2,1)}, bf16[4096,512]{1,0:T(8,128)(2,1)}) fusion(bf16[4096,1024]{1,0:T(8,128)(2,1)} %all-gather.3.cloned.1.call-done), kind=kLoop, calls=%fused_computation.78 | loop fusion | bytes 16777216 | tf_op jit(solution)/shard_map/split | solution.py:50
  100.8 6.4 %copy.83 = bf16[8,512,512]{1,2,0:T(8,128)(2,1)} copy(bf16[8,512,512]{2,1,0:T(8,128)(2,1)} %bitcast.106) | data formatting | bytes 8388608 | tf_op jit(solution)/shard_map/while | solution.py:174
  107.2 6.5 %copy.85 = bf16[8,512,512]{1,2,0:T(8,128)(2,1)} copy(bf16[8,512,512]{2,1,0:T(8,128)(2,1)} %bitcast.105) | data formatting | bytes 8388608 | tf_op jit(solution)/shard_map/while | solution.py:174
  113.9 34.6 %while.24 = (s32[]{:T(128)}, f32[4,6,128]{2,1,0:T(8,128)S(1)}, f32[4,6,128]{2,1,0:T(8,128)S(1)}, f32[4,6,128,128]{3,2,1,0:T(8,128)S(1)}, s32[8,512]{1,0:T(8,128)...) while((s32[]{:T(128)}, f32[4,6,128]{2,1,0:T(8,128)S(1)}, ...), condition=%wide.region_7.8_spmd, body=%wide.region_1.7_spmd.sunk | while | flops 823466496 | bytes 26417920 | solution.py:174
  115.9 6.3 %conditional.4 = (f32[4,6,128]{2,1,0:T(8,128)S(1)}, f32[4,6,128]{2,1,0:T(8,128)S(1)}, f32[4,6,128,128]{3,2,1,0:T(8,128)S(1)}) conditional(s32[]{:T(128)} %convert_element_type.71, (s32[1,512]{1,0:T(1,128)S(1)}, s32[128]{0:T(128)S(1)}, bf16[8,512,512]{1,2,0:T(8,128)(2,1)}, s32[]{:T(128)}, bf16[128,4,6,128]{3,0,2,1:T(8,128)(2,1)S(1)}, ...), branch_computations={%region_3.5_spmd, %region_6.6_spmd} | conditional | flops 823465984 | bytes 26389020 | solution.py:146
  116.0 1.3 constant_dynamic-slice_fusion
  118.5 1.3 fusion.4
  119.8 2.3 multiply_add_fusion
  124.1 6.3 %conditional.4 = (f32[4,6,128]{2,1,0:T(8,128)S(1)}, f32[4,6,128]{2,1,0:T(8,128)S(1)}, f32[4,6,128,128]{3,2,1,0:T(8,128)S(1)}) conditional(s32[]{:T(128)} %convert_element_type.71, (s32[1,512]{1,0:T(1,128)S(1)}, s32[128]{0:T(128)S(1)}, bf16[8,512,512]{1,2,0:T(8,128)(2,1)}, s32[]{:T(128)}, bf16[128,4,6,128]{3,0,2,1:T(8,128)(2,1)S(1)}, ...), branch_computations={%region_3.5_spmd, %region_6.6_spmd} | conditional | flops 823465984 | bytes 26389020 | solution.py:146
  124.2 1.3 constant_dynamic-slice_fusion
  126.7 1.3 fusion.4
  128.0 2.3 multiply_add_fusion
  132.3 6.3 %conditional.4 = (f32[4,6,128]{2,1,0:T(8,128)S(1)}, f32[4,6,128]{2,1,0:T(8,128)S(1)}, f32[4,6,128,128]{3,2,1,0:T(8,128)S(1)}) conditional(s32[]{:T(128)} %convert_element_type.71, (s32[1,512]{1,0:T(1,128)S(1)}, s32[128]{0:T(128)S(1)}, bf16[8,512,512]{1,2,0:T(8,128)(2,1)}, s32[]{:T(128)}, bf16[128,4,6,128]{3,0,2,1:T(8,128)(2,1)S(1)}, ...), branch_computations={%region_3.5_spmd, %region_6.6_spmd} | conditional | flops 823465984 | bytes 26389020 | solution.py:146
  132.5 1.3 constant_dynamic-slice_fusion
  134.9 1.3 fusion.4
  136.3 2.3 multiply_add_fusion
  148.6 1.6 copy.86
  150.2 1.6 broadcast_divide_fusion
  151.8 1.7 fusion.26
  153.5 1.5 fusion.25
  155.1 34.9 %while.25 = (s32[]{:T(128)}, bf16[8,512,512]{2,1,0:T(8,128)(2,1)}, s32[8,512]{1,0:T(8,128)S(1)}, s32[]{:T(128)}, s32[128]{0:T(128)S(1)}, /*index=5*/bf16[8,512,5...) while((s32[]{:T(128)}, bf16[8,512,512]{2,1,0:T(8,128)(2,1)}, ...), condition=%wide.region_12.13_spmd, body=%wide.region_8.12_spmd.sunk | while | flops 811663872 | bytes 5917887 | solution.py:209
  157.0 3.6 %conditional.5 = (bf16[1,512,512]{1,2,0:T(8,128)(2,1)S(1)}) conditional(s32[]{:T(128)} %convert_element_type.72, (s32[1,512]{1,0:T(1,128)S(1)}, s32[128]{0:T(128)S(1)}, bf16[8,512,512]{1,2,0:T(8,128)(2,1)}, s32[]{:T(128)}, bf16[128,4,6,128]{3,0,2,1:T(8,128)(2,1)S(1)}, /*index=5*/f32[4,6,128]{2,1,0:T(8,128)S(1)}, ...), branch_computations={%region_10.10_spmd, %region_11.11_spmd} | conditional | flops 811663360 | bytes 3815948 | solution.py:198
  158.2 2.3 fusion.18
  163.6 3.6 %conditional.5 = (bf16[1,512,512]{1,2,0:T(8,128)(2,1)S(1)}) conditional(s32[]{:T(128)} %convert_element_type.72, (s32[1,512]{1,0:T(1,128)S(1)}, s32[128]{0:T(128)S(1)}, bf16[8,512,512]{1,2,0:T(8,128)(2,1)}, s32[]{:T(128)}, bf16[128,4,6,128]{3,0,2,1:T(8,128)(2,1)S(1)}, /*index=5*/f32[4,6,128]{2,1,0:T(8,128)S(1)}, ...), branch_computations={%region_10.10_spmd, %region_11.11_spmd} | conditional | flops 811663360 | bytes 3815948 | solution.py:198
  164.8 2.3 fusion.18
  170.1 3.6 %conditional.5 = (bf16[1,512,512]{1,2,0:T(8,128)(2,1)S(1)}) conditional(s32[]{:T(128)} %convert_element_type.72, (s32[1,512]{1,0:T(1,128)S(1)}, s32[128]{0:T(128)S(1)}, bf16[8,512,512]{1,2,0:T(8,128)(2,1)}, s32[]{:T(128)}, bf16[128,4,6,128]{3,0,2,1:T(8,128)(2,1)S(1)}, /*index=5*/f32[4,6,128]{2,1,0:T(8,128)S(1)}, ...), branch_computations={%region_10.10_spmd, %region_11.11_spmd} | conditional | flops 811663360 | bytes 3815948 | solution.py:198
  171.4 2.3 fusion.18
  190.0 54.2 %all-to-all-start.1 = ((bf16[32,128,512]{2,1,0:T(8,128)(2,1)}), bf16[32,128,512]{2,1,0:T(8,128)(2,1)}, u32[]{:S(2)}, u32[]{:S(2)}) async-start(bf16[32,128,512]{2,1,0:T(8,128)(2,1)} %bitcast.110), calls=%async_computation.1 | async-start | bytes 8388608 | tf_op jit(solution)/shard_map/all_to_all | solution.py:68
  244.2 4.3 %collective-permute-start.5 = (bf16[128,3072]{0,1:T(8,128)(2,1)S(1)}, bf16[128,3072]{0,1:T(8,128)(2,1)S(1)}, u32[]{:S(2)}, u32[]{:S(2)}) collective-permute-start(bf16[128,3072]{0,1:T(8,128)(2,1)S(1)} %get-tuple-element.429), channel_id=1, source_target_pairs={{1,0},{2,1},{3,2},{4,3},{5,4},{6,5},{7,6},{8,7},{9,8},{10,9},{11,1... | collective-permute-start | bytes 2359304 | tf_op jit(solution)/shard_map/ppermute | solution.py:43
  248.6 53.3 %collective-permute-done.5 = bf16[128,3072]{0,1:T(8,128)(2,1)S(1)} collective-permute-done((bf16[128,3072]{0,1:T(8,128)(2,1)S(1)}, bf16[128,3072]{0,1:T(8,128)(2,1)S(1)}, u32[]{:S(2)}, u32[]{:S(2)}) %collective-permute-start.5) | collective-permute-done | bytes 786464 | tf_op jit(solution)/shard_map/ppermute | solution.py:43
  302.2 1.6 collective-permute-start.6
  303.8 5.7 %collective-permute-start.9 = (bf16[128]{0:T(256)(128)(2,1)S(1)}, bf16[128]{0:T(256)(128)(2,1)S(1)}, u32[]{:S(2)}, u32[]{:S(2)}) collective-permute-start(bf16[128]{0:T(256)(128)(2,1)S(1)} %get-tuple-element.408), channel_id=1, source_target_pairs={{1,0},{2,1},{3,2},{4,3},{5,4},{6,5},{7,6},{8,7},{9,8},{10,9},{11,1... | collective-permute-start | bytes 776 | tf_op jit(solution)/shard_map/ppermute | solution.py:43
  309.5 2.8 reduce_sum.32
  312.3 1.9 collective-permute-start.8
  314.8 25.1 %collective-permute-done.6 = bf16[256,3072]{0,1:T(8,128)(2,1)S(1)} collective-permute-done((bf16[256,3072]{0,1:T(8,128)(2,1)S(1)}, bf16[256,3072]{0,1:T(8,128)(2,1)S(1)}, u32[]{:S(2)}, u32[]{:S(2)}) %collective-permute-start.6) | collective-permute-done | bytes 1572896 | tf_op jit(solution)/shard_map/ppermute | solution.py:74
  339.9 1.7 copy.92
  (138 shorter events, 41.9 us)
Async XLA Ops:
  8.4 15.0 %all-to-all-start = ((s32[32,1,1]{2,1,0:T(1,128)}), s32[32,1,1]{2,1,0:T(1,128)S(1)}, u32[]{:S(2)}, u32[]{:S(2)}) async-start(s32[32,1,1]{2,1,0:T(1,128)} %broadcast_in_dim.73), calls=%async_computation | async-start | bytes 32768 | tf_op jit(solution)/shard_map/all_to_all | solution.py:17
  16.1 79.0 %all-gather.3.cloned.1.call-start = ((), (), s32[]{:S(2)}) async-start(), calls=%async_computation.2 | async-start | bytes 8650752 | tf_op jit(solution)/shard_map/all_gather | solution.py:49
  17.0 9.8 %collective-permute-start.3 = (bf16[128,512]{1,0:T(8,128)(2,1)S(1)}, bf16[128,512]{1,0:T(8,128)(2,1)S(1)}, u32[]{:S(2)}, u32[]{:S(2)}) collective-permute-start(bf16[128,512]{1,0:T(8,128)(2,1)S(1)} %dynamic-slice_bitcast_fusion), channel_id=1, source_target_pairs={{0,1},{1,2},{2,3},{3,4},{4,5},{5,6},{6,7},{7,8},{8,9},{9,10},{10,1... | collective-permute-start | bytes 393224 | tf_op jit(solution)/shard_map/ppermute | solution.py:43
  20.0 8.4 %collective-permute-start.2 = (bf16[128,512]{1,0:T(8,128)(2,1)S(1)}, bf16[128,512]{1,0:T(8,128)(2,1)S(1)}, u32[]{:S(2)}, u32[]{:S(2)}) collective-permute-start(bf16[128,512]{1,0:T(8,128)(2,1)S(1)} %dynamic-slice_bitcast_fusion.1), channel_id=1, source_target_pairs={{0,1},{1,2},{2,3},{3,4},{4,5},{5,6},{6,7},{7,8},{8,9},{9,10},{10,1... | collective-permute-start | bytes 393224 | tf_op jit(solution)/shard_map/ppermute | solution.py:43
  30.0 5.3 %copy-start = (s32[1,256]{1,0:T(1,128)S(1)}, s32[1,256]{1,0:T(1,128)}, u32[]{:S(2)}) copy-start(s32[1,256]{1,0:T(1,128)} %param.20) | copy-start | bytes 3076
  30.1 11.2 %copy-start.1 = (bf16[1,256]{1,0:T(2,128)(2,1)S(1)}, bf16[1,256]{1,0:T(2,128)(2,1)}, u32[]{:S(2)}) copy-start(bf16[1,256]{1,0:T(2,128)(2,1)} %param.19) | copy-start | bytes 1540
  33.4 40.4 %collective-permute-start.4 = (bf16[128,3072]{0,1:T(8,128)(2,1)}, bf16[128,3072]{0,1:T(8,128)(2,1)}, u32[]{:S(2)}, u32[]{:S(2)}) collective-permute-start(bf16[128,3072]{0,1:T(8,128)(2,1)} %bitcast.114), channel_id=1, source_target_pairs={{0,1},{1,2},{2,3},{3,4},{4,5},{5,6},{6,7},{7,8},{8,9},{9,10},{10,1... | collective-permute-start | bytes 2359304 | tf_op jit(solution)/shard_map/ppermute | solution.py:43
  35.4 15.0 %collective-permute-start.1 = (s32[128]{0:T(128)S(1)}, s32[128]{0:T(128)S(1)}, u32[]{:S(2)}, u32[]{:S(2)}) collective-permute-start(s32[128]{0:T(128)S(1)} %fusion.33), channel_id=1, source_target_pairs={{0,1},{1,2},{2,3},{3,4},{4,5},{5,6},{6,7},{7,8},{8,9},{9,10},{10,1... | collective-permute-start | bytes 1544 | tf_op jit(solution)/shard_map/ppermute | solution.py:43
  39.4 112.4 %collective-permute-start.7 = (bf16[128,3072]{0,1:T(8,128)(2,1)}, bf16[128,3072]{0,1:T(8,128)(2,1)}, u32[]{:S(2)}, u32[]{:S(2)}) collective-permute-start(bf16[128,3072]{0,1:T(8,128)(2,1)} %bitcast.33), channel_id=1, source_target_pairs={{0,1},{1,2},{2,3},{3,4},{4,5},{5,6},{6,7},{7,8},{8,9},{9,10},{10,1... | collective-permute-start | bytes 2359304 | tf_op jit(solution)/shard_map/ppermute | solution.py:43
  41.3 112.2 %collective-permute-start = (bf16[128]{0:T(256)(128)(2,1)S(1)}, bf16[128]{0:T(256)(128)(2,1)S(1)}, u32[]{:S(2)}, u32[]{:S(2)}) collective-permute-start(bf16[128]{0:T(256)(128)(2,1)S(1)} %fusion.32), channel_id=1, source_target_pairs={{0,1},{1,2},{2,3},{3,4},{4,5},{5,6},{6,7},{7,8},{8,9},{9,10},{10,1... | collective-permute-start | bytes 776 | tf_op jit(solution)/shard_map/ppermute | solution.py:43
  190.0 119.5 %all-to-all-start.1 = ((bf16[32,128,512]{2,1,0:T(8,128)(2,1)}), bf16[32,128,512]{2,1,0:T(8,128)(2,1)}, u32[]{:S(2)}, u32[]{:S(2)}) async-start(bf16[32,128,512]{2,1,0:T(8,128)(2,1)} %bitcast.110), calls=%async_computation.1 | async-start | bytes 8388608 | tf_op jit(solution)/shard_map/all_to_all | solution.py:68
  244.2 57.7 %collective-permute-start.5 = (bf16[128,3072]{0,1:T(8,128)(2,1)S(1)}, bf16[128,3072]{0,1:T(8,128)(2,1)S(1)}, u32[]{:S(2)}, u32[]{:S(2)}) collective-permute-start(bf16[128,3072]{0,1:T(8,128)(2,1)S(1)} %get-tuple-element.429), channel_id=1, source_target_pairs={{1,0},{2,1},{3,2},{4,3},{5,4},{6,5},{7,6},{8,7},{9,8},{10,9},{11,1... | collective-permute-start | bytes 2359304 | tf_op jit(solution)/shard_map/ppermute | solution.py:43
  302.2 37.8 %collective-permute-start.6 = (bf16[256,3072]{0,1:T(8,128)(2,1)S(1)}, bf16[256,3072]{0,1:T(8,128)(2,1)S(1)}, u32[]{:S(2)}, u32[]{:S(2)}) collective-permute-start(bf16[256,3072]{0,1:T(8,128)(2,1)S(1)} %pad_maximum_fusion), channel_id=1, source_target_pairs={{0,32},{32,64},{64,96},{96,128},{128,160},{160,192},{192,224},{224... | collective-permute-start | bytes 4718600 | tf_op jit(solution)/shard_map/ppermute | solution.py:74
  303.8 10.4 %collective-permute-start.9 = (bf16[128]{0:T(256)(128)(2,1)S(1)}, bf16[128]{0:T(256)(128)(2,1)S(1)}, u32[]{:S(2)}, u32[]{:S(2)}) collective-permute-start(bf16[128]{0:T(256)(128)(2,1)S(1)} %get-tuple-element.408), channel_id=1, source_target_pairs={{1,0},{2,1},{3,2},{4,3},{5,4},{6,5},{7,6},{8,7},{9,8},{10,9},{11,1... | collective-permute-start | bytes 776 | tf_op jit(solution)/shard_map/ppermute | solution.py:43
  312.3 29.3 %collective-permute-start.8 = (bf16[128,512]{1,0:T(8,128)(2,1)S(1)}, bf16[128,512]{1,0:T(8,128)(2,1)S(1)}, u32[]{:S(2)}, u32[]{:S(2)}) collective-permute-start(bf16[128,512]{1,0:T(8,128)(2,1)S(1)} %reduce_sum.32), channel_id=1, source_target_pairs={{1,0},{2,1},{3,2},{4,3},{5,4},{6,5},{7,6},{8,7},{9,8},{10,9},{11,1... | collective-permute-start | bytes 393224 | tf_op jit(solution)/shard_map/ppermute | solution.py:43
Sparse Core Ops, SparseCore 0:
  30.2 64.7 all-gather.2
where the time goes:
time: 351 us; the launch traced here: 349 us
  waiting for transfers between devices  104 us (30%)
  starting transfers between devices  90.6 us (26%)
  local copies, waits for them, and re-layouts  48.6 us (14%)
  other arithmetic  29.5 us (8%)
  blocking collectives  21.7 us (6%)
  loops' own time  21.5 us (6%)
  matrix products  17.3 us (5%)
  between operations  16.4 us (5%)
    ppermute x9, waiting for transfers between devices, passed_along(): return lax.ppermute(block, axis, route)  59.1 us
    all_to_all x1, starting transfers between devices, sent_and_summed(): tiles = lax.all_to_all(in_blocks(x, dim, devices), axis, 0, 0, tiled=True)  54.2 us
    ppermute x9, starting transfers between devices, passed_along(): return lax.ppermute(block, axis, route)  27.1 us
    ppermute x1, waiting for transfers between devices, from_behind(): lax.ppermute(x, axis, [(i, (i + by) % devices) for i in range(devices)])  25.1 us
    all_gather x1, blocking collectives, local(): lax.all_gather(for_sending(place_rows), 'ctx', axis=0, tiled=True)  21.7 us
    all_gather x1, waiting for transfers between devices, sent_together(): out = lax.all_gather(both, axis, axis=dim, tiled=True)  19.5 us
    while x4, local copies, waits for them, and re-layouts, local(): final_state = lax.scan(visit, start_state, stacked)[0]  14.9 us
    another operation x1, loops' own time, local(): final_state = lax.scan(visit, start_state, stacked)[0]  10.5 us
  transfers between devices with their start and end apart: 13, of which 5 were waited for; matrix products, arithmetic and copies ran while one was open for 19% of the time, Pallas kernels for 0%

commit v1 on v0

--- a/solution.py
+++ b/solution.py
@@ -10,6 +10,12 @@
 BLOCK_ROWS = 128
 MAXB = 2
 score_masked_out = -1e30
+
+
+def tiled_gather(x, axis, dim):
+    size = lax.axis_size(axis)
+    repeats = [size if d == dim else 1 for d in range(x.ndim)]
+    return lax.all_to_all(jnp.tile(x, repeats), axis, split_axis=dim, concat_axis=dim, tiled=True)
 
 
 def copy_for_each(x, axis):
@@ -156,7 +162,7 @@
     )
     collected_rows = (
         *sent_together((key_row_block, value_rows), "ctx", 0, 1),
-        lax.all_gather(for_sending(place_rows), "ctx", axis=0, tiled=True).astype(place_rows.dtype),
+        tiled_gather(for_sending(place_rows), "ctx", 0).astype(place_rows.dtype),
     )
     key_complete = collected_rows[0]
     local_row_count = key_complete.shape[0]

time: 351 us -> 353 us (level)
  blocking collectives: 21.7 us -> 0 us
  waiting for transfers between devices: 104 us -> 121 us
  starting transfers between devices: 90.6 us -> 94.6 us
    all_gather x1 -> x0, blocking collectives: 21.7 us -> none  [local(): lax.all_gather(for_sending(place_rows), 'ctx', axis=0, tiled=True)]
    all_gather x1, waiting for transfers between devices: 19.5 us -> 29.3 us  [sent_together(): out = lax.all_gather(both, axis, axis=dim, tiled=True)]
    all_to_all x0 -> x1, starting transfers between devices: none -> 4.97 us  [tiled_gather(): lax.all_to_all(jnp.tile(x, repeats), axis, split_axis=dim, concat_axis=di...]
    ppermute x9, waiting for transfers between devices: 59.1 us -> 63.2 us  [passed_along(): return lax.ppermute(block, axis, route)]
  transfers between devices with their start and end apart: 13 -> 14, of which waited for: 5 -> 6; matrix products, arithmetic and copies ran while one was open for 19% -> 19% of each run, Pallas kernels for 0% -> 0%
where the time goes in v1:
time: 353 us; the launch traced here: 351 us
  waiting for transfers between devices  121 us (34%)
  starting transfers between devices  94.6 us (27%)
  local copies, waits for them, and re-layouts  50.2 us (14%)
  other arithmetic  29.5 us (8%)
  loops' own time  22.4 us (6%)
  matrix products  17.3 us (5%)
  between operations  16.4 us (5%)
    ppermute x9, waiting for transfers between devices, passed_along(): return lax.ppermute(block, axis, route)  63.2 us
    all_to_all x1, starting transfers between devices, sent_and_summed(): tiles = lax.all_to_all(in_blocks(x, dim, devices), axis, 0, 0, tiled=True)  54.2 us
    all_gather x1, waiting for transfers between devices, sent_together(): out = lax.all_gather(both, axis, axis=dim, tiled=True)  29.3 us
    ppermute x9, starting transfers between devices, passed_along(): return lax.ppermute(block, axis, route)  26.2 us
    ppermute x1, waiting for transfers between devices, from_behind(): lax.ppermute(x, axis, [(i, (i + by) % devices) for i in range(devices)])  25.2 us
    while x4, local copies, waits for them, and re-layouts, local(): final_state = lax.scan(visit, start_state, stacked)[0]  15 us
    another operation x1, loops' own time, local(): final_state = lax.scan(visit, start_state, stacked)[0]  11 us
    another operation x1, loops' own time, local(): lax.map(lambda member: value_block(member[0], member[1]), (key_portion.re...  10.9 us
  transfers between devices with their start and end apart: 14, of which 6 were waited for; matrix products, arithmetic and copies ran while one was open for 19% of the time, Pallas kernels for 0%

profile of v1, /device:TPU:2, one launch (start us, length us, event | category | flops | bytes accessed | tf_op | source)
XLA Modules:
  0.0 351.3 jit_solution(9729828805899443754)
XLA Ops:
  8.4 7.6 %all-to-all-start = ((s32[32,1,1]{2,1,0:T(1,128)}), s32[32,1,1]{2,1,0:T(1,128)S(1)}, u32[]{:S(2)}, u32[]{:S(2)}) async-start(s32[32,1,1]{2,1,0:T(1,128)} %broadcast_in_dim.73), calls=%async_computation | async-start | bytes 32768 | tf_op jit(solution)/shard_map/all_to_all | solution.py:23
  17.0 2.0 collective-permute-start.3
  20.0 3.4 collective-permute-start.2
  30.1 2.3 fusion.39
  33.5 1.9 collective-permute-start.4
  35.5 2.8 collective-permute-start.1
  39.5 1.9 collective-permute-start.7
  41.4 9.2 %collective-permute-done.1 = s32[128]{0:T(128)S(1)} collective-permute-done((s32[128]{0:T(128)S(1)}, s32[128]{0:T(128)S(1)}, u32[]{:S(2)}, u32[]{:S(2)}) %collective-permute-start.1) | collective-permute-done | bytes 544 | tf_op jit(solution)/shard_map/ppermute | solution.py:49
  51.9 5.0 %all-to-all-start.1 = ((s32[32,128,1]{1,2,0:T(1,128)}), s32[32,128,1]{1,2,0:T(1,128)S(1)}, u32[]{:S(2)}, u32[]{:S(2)}) async-start(s32[32,128,1]{1,2,0:T(1,128)} %all_to_all.17), calls=%async_computation.1 | async-start | bytes 32768 | tf_op jit(solution)/shard_map/all_to_all | solution.py:18
  56.9 2.2 collective-permute-start
  59.9 3.2 all-to-all-done.1
  65.9 29.3 %all-gather.2.cloned.1.call-done = bf16[4096,1024]{1,0:T(8,128)(2,1)} async-done(((bf16[128,1024]{1,0:T(8,128)(2,1)}), bf16[4096,1024]{1,0:T(8,128)(2,1)}) %all-gather.2.cloned.1.call-update) | async-done | bytes 8388624 | tf_op jit(solution)/shard_map/all_gather | solution.py:55
  95.2 5.8 %fusion.38 = (bf16[4096,512]{1,0:T(8,128)(2,1)}, bf16[4096,512]{1,0:T(8,128)(2,1)}) fusion(bf16[4096,1024]{1,0:T(8,128)(2,1)} %all-gather.2.cloned.1.call-done), kind=kLoop, calls=%fused_computation.78 | loop fusion | bytes 16777216 | tf_op jit(solution)/shard_map/split | solution.py:56
  100.9 6.5 %copy.83 = bf16[8,512,512]{1,2,0:T(8,128)(2,1)} copy(bf16[8,512,512]{2,1,0:T(8,128)(2,1)} %bitcast.106) | data formatting | bytes 8388608 | tf_op jit(solution)/shard_map/while | solution.py:180
  107.4 6.5 %copy.85 = bf16[8,512,512]{1,2,0:T(8,128)(2,1)} copy(bf16[8,512,512]{2,1,0:T(8,128)(2,1)} %bitcast.105) | data formatting | bytes 8388608 | tf_op jit(solution)/shard_map/while | solution.py:180
  114.1 35.1 %while.24 = (s32[]{:T(128)}, f32[4,6,128]{2,1,0:T(8,128)S(1)}, f32[4,6,128]{2,1,0:T(8,128)S(1)}, f32[4,6,128,128]{3,2,1,0:T(8,128)S(1)}, s32[8,512]{1,0:T(8,128)...) while((s32[]{:T(128)}, f32[4,6,128]{2,1,0:T(8,128)S(1)}, ...), condition=%wide.region_7.8_spmd, body=%wide.region_1.7_spmd.sunk | while | flops 823466496 | bytes 26417920 | solution.py:180
  116.1 6.3 %conditional.4 = (f32[4,6,128]{2,1,0:T(8,128)S(1)}, f32[4,6,128]{2,1,0:T(8,128)S(1)}, f32[4,6,128,128]{3,2,1,0:T(8,128)S(1)}) conditional(s32[]{:T(128)} %convert_element_type.71, (s32[1,512]{1,0:T(1,128)S(1)}, s32[128]{0:T(128)S(1)}, bf16[8,512,512]{1,2,0:T(8,128)(2,1)}, s32[]{:T(128)}, bf16[128,4,6,128]{3,0,2,1:T(8,128)(2,1)S(1)}, ...), branch_computations={%region_3.5_spmd, %region_6.6_spmd} | conditional | flops 823465984 | bytes 26389020 | solution.py:152
  116.2 1.3 constant_dynamic-slice_fusion
  118.7 1.3 fusion.4
  120.0 2.3 multiply_add_fusion
  124.4 6.3 %conditional.4 = (f32[4,6,128]{2,1,0:T(8,128)S(1)}, f32[4,6,128]{2,1,0:T(8,128)S(1)}, f32[4,6,128,128]{3,2,1,0:T(8,128)S(1)}) conditional(s32[]{:T(128)} %convert_element_type.71, (s32[1,512]{1,0:T(1,128)S(1)}, s32[128]{0:T(128)S(1)}, bf16[8,512,512]{1,2,0:T(8,128)(2,1)}, s32[]{:T(128)}, bf16[128,4,6,128]{3,0,2,1:T(8,128)(2,1)S(1)}, ...), branch_computations={%region_3.5_spmd, %region_6.6_spmd} | conditional | flops 823465984 | bytes 26389020 | solution.py:152
  124.5 1.3 constant_dynamic-slice_fusion
  127.0 1.3 fusion.4
  128.3 2.3 multiply_add_fusion
  132.6 6.3 %conditional.4 = (f32[4,6,128]{2,1,0:T(8,128)S(1)}, f32[4,6,128]{2,1,0:T(8,128)S(1)}, f32[4,6,128,128]{3,2,1,0:T(8,128)S(1)}) conditional(s32[]{:T(128)} %convert_element_type.71, (s32[1,512]{1,0:T(1,128)S(1)}, s32[128]{0:T(128)S(1)}, bf16[8,512,512]{1,2,0:T(8,128)(2,1)}, s32[]{:T(128)}, bf16[128,4,6,128]{3,0,2,1:T(8,128)(2,1)S(1)}, ...), branch_computations={%region_3.5_spmd, %region_6.6_spmd} | conditional | flops 823465984 | bytes 26389020 | solution.py:152
  132.8 1.3 constant_dynamic-slice_fusion
  135.3 1.3 fusion.4
  136.6 2.3 multiply_add_fusion
  149.2 1.6 copy.86
  150.8 1.6 broadcast_divide_fusion
  152.4 1.7 fusion.26
  154.2 1.5 fusion.25
  155.7 35.4 %while.25 = (s32[]{:T(128)}, bf16[8,512,512]{2,1,0:T(8,128)(2,1)}, s32[8,512]{1,0:T(8,128)S(1)}, s32[]{:T(128)}, s32[128]{0:T(128)S(1)}, /*index=5*/bf16[8,512,5...) while((s32[]{:T(128)}, bf16[8,512,512]{2,1,0:T(8,128)(2,1)}, ...), condition=%wide.region_12.13_spmd, body=%wide.region_8.12_spmd.sunk | while | flops 811663872 | bytes 5917887 | solution.py:215
  157.7 3.6 %conditional.5 = (bf16[1,512,512]{1,2,0:T(8,128)(2,1)S(1)}) conditional(s32[]{:T(128)} %convert_element_type.72, (s32[1,512]{1,0:T(1,128)S(1)}, s32[128]{0:T(128)S(1)}, bf16[8,512,512]{1,2,0:T(8,128)(2,1)}, s32[]{:T(128)}, bf16[128,4,6,128]{3,0,2,1:T(8,128)(2,1)S(1)}, /*index=5*/f32[4,6,128]{2,1,0:T(8,128)S(1)}, ...), branch_computations={%region_10.10_spmd, %region_11.11_spmd} | conditional | flops 811663360 | bytes 3815948 | solution.py:204
  158.9 2.3 fusion.18
  164.3 3.6 %conditional.5 = (bf16[1,512,512]{1,2,0:T(8,128)(2,1)S(1)}) conditional(s32[]{:T(128)} %convert_element_type.72, (s32[1,512]{1,0:T(1,128)S(1)}, s32[128]{0:T(128)S(1)}, bf16[8,512,512]{1,2,0:T(8,128)(2,1)}, s32[]{:T(128)}, bf16[128,4,6,128]{3,0,2,1:T(8,128)(2,1)S(1)}, /*index=5*/f32[4,6,128]{2,1,0:T(8,128)S(1)}, ...), branch_computations={%region_10.10_spmd, %region_11.11_spmd} | conditional | flops 811663360 | bytes 3815948 | solution.py:204
  165.5 2.3 fusion.18
  170.9 3.6 %conditional.5 = (bf16[1,512,512]{1,2,0:T(8,128)(2,1)S(1)}) conditional(s32[]{:T(128)} %convert_element_type.72, (s32[1,512]{1,0:T(1,128)S(1)}, s32[128]{0:T(128)S(1)}, bf16[8,512,512]{1,2,0:T(8,128)(2,1)}, s32[]{:T(128)}, bf16[128,4,6,128]{3,0,2,1:T(8,128)(2,1)S(1)}, /*index=5*/f32[4,6,128]{2,1,0:T(8,128)S(1)}, ...), branch_computations={%region_10.10_spmd, %region_11.11_spmd} | conditional | flops 811663360 | bytes 3815948 | solution.py:204
  172.2 2.3 fusion.18
  191.1 54.2 %all-to-all-start.2 = ((bf16[32,128,512]{2,1,0:T(8,128)(2,1)}), bf16[32,128,512]{2,1,0:T(8,128)(2,1)}, u32[]{:S(2)}, u32[]{:S(2)}) async-start(bf16[32,128,512]{2,1,0:T(8,128)(2,1)} %bitcast.110), calls=%async_computation.2 | async-start | bytes 8388608 | tf_op jit(solution)/shard_map/all_to_all | solution.py:74
  245.3 4.3 %collective-permute-start.5 = (bf16[128,3072]{0,1:T(8,128)(2,1)S(1)}, bf16[128,3072]{0,1:T(8,128)(2,1)S(1)}, u32[]{:S(2)}, u32[]{:S(2)}) collective-permute-start(bf16[128,3072]{0,1:T(8,128)(2,1)S(1)} %get-tuple-element.429), channel_id=1, source_target_pairs={{1,0},{2,1},{3,2},{4,3},{5,4},{6,5},{7,6},{8,7},{9,8},{10,9},{11,1... | collective-permute-start | bytes 2359304 | tf_op jit(solution)/shard_map/ppermute | solution.py:49
  249.6 53.3 %collective-permute-done.5 = bf16[128,3072]{0,1:T(8,128)(2,1)S(1)} collective-permute-done((bf16[128,3072]{0,1:T(8,128)(2,1)S(1)}, bf16[128,3072]{0,1:T(8,128)(2,1)S(1)}, u32[]{:S(2)}, u32[]{:S(2)}) %collective-permute-start.5) | collective-permute-done | bytes 786464 | tf_op jit(solution)/shard_map/ppermute | solution.py:49
  303.2 1.6 collective-permute-start.6
  304.9 5.7 %collective-permute-start.9 = (bf16[128]{0:T(256)(128)(2,1)S(1)}, bf16[128]{0:T(256)(128)(2,1)S(1)}, u32[]{:S(2)}, u32[]{:S(2)}) collective-permute-start(bf16[128]{0:T(256)(128)(2,1)S(1)} %get-tuple-element.408), channel_id=1, source_target_pairs={{1,0},{2,1},{3,2},{4,3},{5,4},{6,5},{7,6},{8,7},{9,8},{10,9},{11,1... | collective-permute-start | bytes 776 | tf_op jit(solution)/shard_map/ppermute | solution.py:49
  310.6 2.8 reduce_sum.32
  313.4 1.9 collective-permute-start.8
  315.9 25.2 %collective-permute-done.6 = bf16[256,3072]{0,1:T(8,128)(2,1)} collective-permute-done((bf16[256,3072]{0,1:T(8,128)(2,1)S(1)}, bf16[256,3072]{0,1:T(8,128)(2,1)}, u32[]{:S(2)}, u32[]{:S(2)}) %collective-permute-start.6) | collective-permute-done | bytes 1572896 | tf_op jit(solution)/shard_map/ppermute | solution.py:80
  341.1 2.6 copy.92
  (140 shorter events, 43.7 us)
Async XLA Ops:
  8.4 15.0 %all-to-all-start = ((s32[32,1,1]{2,1,0:T(1,128)}), s32[32,1,1]{2,1,0:T(1,128)S(1)}, u32[]{:S(2)}, u32[]{:S(2)}) async-start(s32[32,1,1]{2,1,0:T(1,128)} %broadcast_in_dim.73), calls=%async_computation | async-start | bytes 32768 | tf_op jit(solution)/shard_map/all_to_all | solution.py:23
  16.1 79.1 %all-gather.2.cloned.1.call-start = ((), (), s32[]{:S(2)}) async-start(), calls=%async_computation.3 | async-start | bytes 8650752 | tf_op jit(solution)/shard_map/all_gather | solution.py:55
  17.0 9.8 %collective-permute-start.3 = (bf16[128,512]{1,0:T(8,128)(2,1)S(1)}, bf16[128,512]{1,0:T(8,128)(2,1)S(1)}, u32[]{:S(2)}, u32[]{:S(2)}) collective-permute-start(bf16[128,512]{1,0:T(8,128)(2,1)S(1)} %dynamic-slice_bitcast_fusion), channel_id=1, source_target_pairs={{0,1},{1,2},{2,3},{3,4},{4,5},{5,6},{6,7},{7,8},{8,9},{9,10},{10,1... | collective-permute-start | bytes 393224 | tf_op jit(solution)/shard_map/ppermute | solution.py:49
  20.0 8.4 %collective-permute-start.2 = (bf16[128,512]{1,0:T(8,128)(2,1)S(1)}, bf16[128,512]{1,0:T(8,128)(2,1)S(1)}, u32[]{:S(2)}, u32[]{:S(2)}) collective-permute-start(bf16[128,512]{1,0:T(8,128)(2,1)S(1)} %dynamic-slice_bitcast_fusion.1), channel_id=1, source_target_pairs={{0,1},{1,2},{2,3},{3,4},{4,5},{5,6},{6,7},{7,8},{8,9},{9,10},{10,1... | collective-permute-start | bytes 393224 | tf_op jit(solution)/shard_map/ppermute | solution.py:49
  30.0 5.4 %copy-start = (s32[1,256]{1,0:T(1,128)S(1)}, s32[1,256]{1,0:T(1,128)}, u32[]{:S(2)}) copy-start(s32[1,256]{1,0:T(1,128)} %param.20) | copy-start | bytes 3076
  30.1 26.8 %copy-start.1 = (bf16[1,256]{1,0:T(2,128)(2,1)S(1)}, bf16[1,256]{1,0:T(2,128)(2,1)}, u32[]{:S(2)}) copy-start(bf16[1,256]{1,0:T(2,128)(2,1)} %param.19) | copy-start | bytes 1540
  33.5 30.7 %collective-permute-start.4 = (bf16[128,3072]{0,1:T(8,128)(2,1)}, bf16[128,3072]{0,1:T(8,128)(2,1)}, u32[]{:S(2)}, u32[]{:S(2)}) collective-permute-start(bf16[128,3072]{0,1:T(8,128)(2,1)} %bitcast.113), channel_id=1, source_target_pairs={{0,1},{1,2},{2,3},{3,4},{4,5},{5,6},{6,7},{7,8},{8,9},{9,10},{10,1... | collective-permute-start | bytes 2359304 | tf_op jit(solution)/shard_map/ppermute | solution.py:49
  35.5 15.1 %collective-permute-start.1 = (s32[128]{0:T(128)S(1)}, s32[128]{0:T(128)S(1)}, u32[]{:S(2)}, u32[]{:S(2)}) collective-permute-start(s32[128]{0:T(128)S(1)} %fusion.33), channel_id=1, source_target_pairs={{0,1},{1,2},{2,3},{3,4},{4,5},{5,6},{6,7},{7,8},{8,9},{9,10},{10,1... | collective-permute-start | bytes 1544 | tf_op jit(solution)/shard_map/ppermute | solution.py:49
  39.5 112.9 %collective-permute-start.7 = (bf16[128,3072]{0,1:T(8,128)(2,1)}, bf16[128,3072]{0,1:T(8,128)(2,1)}, u32[]{:S(2)}, u32[]{:S(2)}) collective-permute-start(bf16[128,3072]{0,1:T(8,128)(2,1)} %bitcast.32), channel_id=1, source_target_pairs={{0,1},{1,2},{2,3},{3,4},{4,5},{5,6},{6,7},{7,8},{8,9},{9,10},{10,1... | collective-permute-start | bytes 2359304 | tf_op jit(solution)/shard_map/ppermute | solution.py:49
  51.9 11.2 %all-to-all-start.1 = ((s32[32,128,1]{1,2,0:T(1,128)}), s32[32,128,1]{1,2,0:T(1,128)S(1)}, u32[]{:S(2)}, u32[]{:S(2)}) async-start(s32[32,128,1]{1,2,0:T(1,128)} %all_to_all.17), calls=%async_computation.1 | async-start | bytes 32768 | tf_op jit(solution)/shard_map/all_to_all | solution.py:18
  56.9 97.2 %collective-permute-start = (bf16[128]{0:T(256)(128)(2,1)S(1)}, bf16[128]{0:T(256)(128)(2,1)S(1)}, u32[]{:S(2)}, u32[]{:S(2)}) collective-permute-start(bf16[128]{0:T(256)(128)(2,1)S(1)} %fusion.32), channel_id=1, source_target_pairs={{0,1},{1,2},{2,3},{3,4},{4,5},{5,6},{6,7},{7,8},{8,9},{9,10},{10,1... | collective-permute-start | bytes 776 | tf_op jit(solution)/shard_map/ppermute | solution.py:49
  191.1 119.5 %all-to-all-start.2 = ((bf16[32,128,512]{2,1,0:T(8,128)(2,1)}), bf16[32,128,512]{2,1,0:T(8,128)(2,1)}, u32[]{:S(2)}, u32[]{:S(2)}) async-start(bf16[32,128,512]{2,1,0:T(8,128)(2,1)} %bitcast.110), calls=%async_computation.2 | async-start | bytes 8388608 | tf_op jit(solution)/shard_map/all_to_all | solution.py:74
  245.3 57.7 %collective-permute-start.5 = (bf16[128,3072]{0,1:T(8,128)(2,1)S(1)}, bf16[128,3072]{0,1:T(8,128)(2,1)S(1)}, u32[]{:S(2)}, u32[]{:S(2)}) collective-permute-start(bf16[128,3072]{0,1:T(8,128)(2,1)S(1)} %get-tuple-element.429), channel_id=1, source_target_pairs={{1,0},{2,1},{3,2},{4,3},{5,4},{6,5},{7,6},{8,7},{9,8},{10,9},{11,1... | collective-permute-start | bytes 2359304 | tf_op jit(solution)/shard_map/ppermute | solution.py:49
  303.2 37.9 %collective-permute-start.6 = (bf16[256,3072]{0,1:T(8,128)(2,1)S(1)}, bf16[256,3072]{0,1:T(8,128)(2,1)}, u32[]{:S(2)}, u32[]{:S(2)}) collective-permute-start(bf16[256,3072]{0,1:T(8,128)(2,1)S(1)} %pad_maximum_fusion), channel_id=1, source_target_pairs={{0,32},{32,64},{64,96},{96,128},{128,160},{160,192},{192,224},{224... | collective-permute-start | bytes 4718600 | tf_op jit(solution)/shard_map/ppermute | solution.py:80
  304.9 10.4 %collective-permute-start.9 = (bf16[128]{0:T(256)(128)(2,1)S(1)}, bf16[128]{0:T(256)(128)(2,1)S(1)}, u32[]{:S(2)}, u32[]{:S(2)}) collective-permute-start(bf16[128]{0:T(256)(128)(2,1)S(1)} %get-tuple-element.408), channel_id=1, source_target_pairs={{1,0},{2,1},{3,2},{4,3},{5,4},{6,5},{7,6},{8,7},{9,8},{10,9},{11,1... | collective-permute-start | bytes 776 | tf_op jit(solution)/shard_map/ppermute | solution.py:49
  313.4 30.3 %collective-permute-start.8 = (bf16[128,512]{1,0:T(8,128)(2,1)S(1)}, bf16[128,512]{1,0:T(8,128)(2,1)S(1)}, u32[]{:S(2)}, u32[]{:S(2)}) collective-permute-start(bf16[128,512]{1,0:T(8,128)(2,1)S(1)} %reduce_sum.32), channel_id=1, source_target_pairs={{1,0},{2,1},{3,2},{4,3},{5,4},{6,5},{7,6},{8,7},{9,8},{10,9},{11,1... | collective-permute-start | bytes 393224 | tf_op jit(solution)/shard_map/ppermute | solution.py:49
Sparse Core Ops, SparseCore 0:
  30.2 64.9 all-gather.1
